TPU v7x, 32 devices: a whole 2x2x4 slice. The times are simulated.
32 devices in a mesh: blk: 4 (over y, x), tok: 8 (over z, core).
Axes of the slice: x: 2, y: 2, z: 4, core: 2. Of those that a mesh axis runs over, the one named last changes fastest.
Arguments:
- states: bfloat16 [256, 3584], P('tok'), may hold values from -30 to 30
- head: bfloat16 [3584, 32768], P(None, ('blk', 'tok')), may hold values from -0.2 to 0.2
- targets: int32 [256], P('tok'), may hold values from 0 to 32767
- ref_loss: float32 [256], P('tok'), may hold values from 0 to 8
- seq_ids: int32 [256], P('tok'), may hold values from 0 to 127, never falling along the last dimension, each value on 1 to 4 neighbouring positions
Outputs:
- excess: float32 [256], P('tok')
- seq_score: float32 [128], replicated
Inputs may be any that keep to these rules, and one draw needn't show every extreme that they name: `seq_ids`: sequence numbers never fall along the tokens; every number from 0 to 127 occurs, on 1 to 4 consecutive tokens.
All inputs are finite; a program needn't handle non-finite values.
Results may differ from a plain program's by a relative error of at most 0.0003.
Values may be sent and summed in bfloat16 or wider, within the bound.
A program may use at most 64 MiB of HBM per device.

v0:
```python
import jax
import jax.numpy as jnp
from jax import lax
from jax.sharding import PartitionSpec as P

very_low = -1e30


def from_behind(value, axis, by):
    devices = lax.axis_size(axis)
    return lax.ppermute(value, axis, [(i, (i + by) % devices) for i in range(devices)])


def merged(value, axis, join):
    pieces = jax.tree.map(lambda part: lax.all_gather(part, axis), value)
    head = jax.tree.map(lambda part: part[0], pieces)
    tail = jax.tree.map(lambda part: part[1:], pieces)
    so_far, _ = lax.scan(lambda so_far, section: (join(so_far, section), None), head, tail)
    return so_far


def absorb(highest, scaled, picked, token_rows, target_ids, head, first_col):
    logits = jnp.dot(token_rows, head, preferred_element_type=jnp.float32)
    new_high = jnp.maximum(highest, jnp.max(logits, axis=1))
    scaled = scaled * jnp.exp(highest - new_high) + jnp.sum(
        jnp.exp(logits - new_high[:, None]), axis=1
    )
    columns = first_col + lax.iota(jnp.int32, head.shape[1])
    hits = columns[None, :] == target_ids[:, None]
    picked = picked + jnp.sum(jnp.where(hits, logits, 0.0), axis=1)
    return (new_high, scaled, picked)


def combine_stats(left, right):
    left_high, left_scaled, left_picked = left
    right_high, right_scaled, right_picked = right
    highest = jnp.maximum(left_high, right_high)
    scaled = left_scaled * jnp.exp(left_high - highest) + right_scaled * jnp.exp(
        right_high - highest
    )
    return (highest, scaled, left_picked + right_picked)


def on_device(states, head, targets, ref_loss, seq_ids):
    cycle_size = lax.axis_size("tok")
    first_col = (lax.axis_index("blk") * cycle_size + lax.axis_index("tok")) * head.shape[1]
    local = states.shape[0]

    def advance(step, carried):
        token_rows, target_ids, highest, scaled, picked = carried
        highest, scaled, picked = absorb(
            highest, scaled, picked, token_rows, target_ids, head, first_col
        )
        token_rows, target_ids = from_behind((token_rows, target_ids), "tok", 1)
        highest, scaled, picked = from_behind((highest, scaled, picked), "tok", 1)
        return (token_rows, target_ids, highest, scaled, picked)

    begin = (
        states,
        targets,
        jnp.full((local,), very_low, jnp.float32),
        jnp.zeros((local,), jnp.float32),
        jnp.zeros((local,), jnp.float32),
    )
    token_rows, target_ids, highest, scaled, picked = lax.fori_loop(
        0, cycle_size - 1, advance, begin
    )
    highest, scaled, picked = absorb(
        highest, scaled, picked, token_rows, target_ids, head, first_col
    )
    highest, scaled, picked = from_behind((highest, scaled, picked), "tok", 1)
    highest, scaled, picked = merged((highest, scaled, picked), "blk", combine_stats)
    excess = highest + jnp.log(scaled) - picked - ref_loss
    seq_count = local * cycle_size // 2
    member = (seq_ids[:, None] == lax.iota(jnp.int32, seq_count)[None, :]).astype(jnp.float32)
    totals = jnp.dot(excess, member, precision=lax.Precision.HIGHEST)
    counts = jnp.sum(member, axis=0)
    totals, counts = lax.psum((totals, counts), "tok")
    return (excess, totals / counts)


def solution(mesh):
    placed = (P("tok", None), P(None, ("blk", "tok")), P("tok"), P("tok"), P("tok"))
    return jax.shard_map(
        on_device, mesh=mesh, in_specs=placed, out_specs=(P("tok"), P()), check_vma=False
    )
```

profile of v0, /device:TPU:0, one launch (start us, length us, event | category | flops | bytes accessed | tf_op | source)
XLA Modules:
  0.0 121.7 jit_solution(972116831383671093)
XLA Ops:
  0.6 0.9 copy.43
  1.6 0.7 copy.44
  2.2 84.2 %while.32 = (s32[]{:T(128)}, bf16[32,3584]{1,0:T(8,128)(2,1)S(1)}, s32[32]{0:T(128)S(1)}, f32[32]{0:T(128)S(1)}, f32[32]{0:T(128)S(1)}, /*index=5*/f32[32]{0:T(1...) while((s32[]{:T(128)}, bf16[32,3584]{1,0:T(8,128)(2,1)S(1)}, s32[32]{0:T(128)S(1)}, f32[32]{0:T(128)S(1)}, ...), condition=%wide.region_4.5_spmd, body=%wide.region_0.4_spmd.sunk | while | flops 235078720 | bytes 9220905 | solution.py:65
  2.3 0.5 collective-permute-start
  2.8 4.6 %fusion.22 = (f32[32]{0:T(128)S(1)}, f32[32,1024]{1,0:T(8,128)S(1)}) fusion(bf16[32,3584]{1,0:T(8,128)(2,1)S(1)} %copy.14, bf16[3584,1024]{1,0:T(8,128)(2,1)} %get-tuple-element.271), kind=kOutput, calls=%fused_computation.24.clone.1 | convolution fusion | flops 234913760 | bytes 7700608 | tf_op jit(solution)/shard_map/while/body/eval_jaxpr/dot_general | solution.py:23
  7.4 2.7 %collective-permute-start.2 = (f32[32]{0:T(128)S(1)}, f32[32]{0:T(128)S(1)}, u32[]{:S(2)}, u32[]{:S(2)}) collective-permute-start(f32[32]{0:T(128)S(1)} %max.13), channel_id=1, source_target_pairs={{0,1},{1,2},{2,3},{3,4},{4,5},{5,6},{6,7},{7,0},{8,9},{9,10},{10,1... | collective-permute-start | bytes 392 | tf_op jit(solution)/shard_map/while/body/eval_jaxpr/ppermute | solution.py:11
  10.2 0.2 select_reduce_fusion.3
  10.4 1.7 %collective-permute-start.3 = (f32[32]{0:T(128)S(1)}, f32[32]{0:T(128)S(1)}, u32[]{:S(2)}, u32[]{:S(2)}) collective-permute-start(f32[32]{0:T(128)S(1)} %multiply_add_fusion.3), channel_id=1, source_target_pairs={{0,1},{1,2},{2,3},{3,4},{4,5},{5,6},{6,7},{7,0},{8,9},{9,10},{10,1... | collective-permute-start | bytes 392 | tf_op jit(solution)/shard_map/while/body/eval_jaxpr/ppermute | solution.py:11
  12.1 0.6 collective-permute-done.2
  12.7 2.5 %collective-permute-done.3 = f32[32]{0:T(128)S(1)} collective-permute-done((f32[32]{0:T(128)S(1)}, f32[32]{0:T(128)S(1)}, u32[]{:S(2)}, u32[]{:S(2)}) %collective-permute-start.3) | collective-permute-done | bytes 160 | tf_op jit(solution)/shard_map/while/body/eval_jaxpr/ppermute | solution.py:11
  15.2 1.6 %collective-permute-done.4 = f32[32]{0:T(128)S(1)} collective-permute-done((f32[32]{0:T(128)S(1)}, f32[32]{0:T(128)S(1)}, u32[]{:S(2)}, u32[]{:S(2)}) %collective-permute-start.4) | collective-permute-done | bytes 160 | tf_op jit(solution)/shard_map/while/body/eval_jaxpr/ppermute | solution.py:11
  17.0 4.6 %fusion.22 = (f32[32]{0:T(128)S(1)}, f32[32,1024]{1,0:T(8,128)S(1)}) fusion(bf16[32,3584]{1,0:T(8,128)(2,1)S(1)} %copy.14, bf16[3584,1024]{1,0:T(8,128)(2,1)} %get-tuple-element.271), kind=kOutput, calls=%fused_computation.24.clone.1 | convolution fusion | flops 234913760 | bytes 7700608 | tf_op jit(solution)/shard_map/while/body/eval_jaxpr/dot_general | solution.py:23
  21.7 0.2 select_reduce_fusion.3
  22.1 4.3 %collective-permute-done.2 = f32[32]{0:T(128)S(1)} collective-permute-done((f32[32]{0:T(128)S(1)}, f32[32]{0:T(128)S(1)}, u32[]{:S(2)}, u32[]{:S(2)}) %collective-permute-start.2) | collective-permute-done | bytes 160 | tf_op jit(solution)/shard_map/while/body/eval_jaxpr/ppermute | solution.py:11
  26.4 0.4 collective-permute-done.3
  26.8 0.2 collective-permute-done.4
  27.0 4.6 %fusion.22 = (f32[32]{0:T(128)S(1)}, f32[32,1024]{1,0:T(8,128)S(1)}) fusion(bf16[32,3584]{1,0:T(8,128)(2,1)S(1)} %copy.14, bf16[3584,1024]{1,0:T(8,128)(2,1)} %get-tuple-element.271), kind=kOutput, calls=%fused_computation.24.clone.1 | convolution fusion | flops 234913760 | bytes 7700608 | tf_op jit(solution)/shard_map/while/body/eval_jaxpr/dot_general | solution.py:23
  31.7 1.0 collective-permute-start.1
  32.7 0.2 select_reduce_fusion.3
  32.9 2.3 %collective-permute-start.3 = (f32[32]{0:T(128)S(1)}, f32[32]{0:T(128)S(1)}, u32[]{:S(2)}, u32[]{:S(2)}) collective-permute-start(f32[32]{0:T(128)S(1)} %multiply_add_fusion.3), channel_id=1, source_target_pairs={{0,1},{1,2},{2,3},{3,4},{4,5},{5,6},{6,7},{7,0},{8,9},{9,10},{10,1... | collective-permute-start | bytes 392 | tf_op jit(solution)/shard_map/while/body/eval_jaxpr/ppermute | solution.py:11
  35.3 1.1 collective-permute-done.2
  36.4 1.3 %collective-permute-done.3 = f32[32]{0:T(128)S(1)} collective-permute-done((f32[32]{0:T(128)S(1)}, f32[32]{0:T(128)S(1)}, u32[]{:S(2)}, u32[]{:S(2)}) %collective-permute-start.3) | collective-permute-done | bytes 160 | tf_op jit(solution)/shard_map/while/body/eval_jaxpr/ppermute | solution.py:11
  37.8 2.3 %collective-permute-done.4 = f32[32]{0:T(128)S(1)} collective-permute-done((f32[32]{0:T(128)S(1)}, f32[32]{0:T(128)S(1)}, u32[]{:S(2)}, u32[]{:S(2)}) %collective-permute-start.4) | collective-permute-done | bytes 160 | tf_op jit(solution)/shard_map/while/body/eval_jaxpr/ppermute | solution.py:11
  40.1 4.6 %fusion.22 = (f32[32]{0:T(128)S(1)}, f32[32,1024]{1,0:T(8,128)S(1)}) fusion(bf16[32,3584]{1,0:T(8,128)(2,1)S(1)} %copy.14, bf16[3584,1024]{1,0:T(8,128)(2,1)} %get-tuple-element.271), kind=kOutput, calls=%fused_computation.24.clone.1 | convolution fusion | flops 234913760 | bytes 7700608 | tf_op jit(solution)/shard_map/while/body/eval_jaxpr/dot_general | solution.py:23
  44.9 0.2 select_reduce_fusion.3
  45.1 0.2 collective-permute-start.3
  45.4 4.2 %collective-permute-done.2 = f32[32]{0:T(128)S(1)} collective-permute-done((f32[32]{0:T(128)S(1)}, f32[32]{0:T(128)S(1)}, u32[]{:S(2)}, u32[]{:S(2)}) %collective-permute-start.2) | collective-permute-done | bytes 160 | tf_op jit(solution)/shard_map/while/body/eval_jaxpr/ppermute | solution.py:11
  49.5 0.4 collective-permute-done.3
  49.9 0.2 collective-permute-done.4
  50.2 4.6 %fusion.22 = (f32[32]{0:T(128)S(1)}, f32[32,1024]{1,0:T(8,128)S(1)}) fusion(bf16[32,3584]{1,0:T(8,128)(2,1)S(1)} %copy.14, bf16[3584,1024]{1,0:T(8,128)(2,1)} %get-tuple-element.271), kind=kOutput, calls=%fused_computation.24.clone.1 | convolution fusion | flops 234913760 | bytes 7700608 | tf_op jit(solution)/shard_map/while/body/eval_jaxpr/dot_general | solution.py:23
  54.8 1.0 collective-permute-start.1
  55.9 0.2 select_reduce_fusion.3
  56.1 2.3 %collective-permute-start.3 = (f32[32]{0:T(128)S(1)}, f32[32]{0:T(128)S(1)}, u32[]{:S(2)}, u32[]{:S(2)}) collective-permute-start(f32[32]{0:T(128)S(1)} %multiply_add_fusion.3), channel_id=1, source_target_pairs={{0,1},{1,2},{2,3},{3,4},{4,5},{5,6},{6,7},{7,0},{8,9},{9,10},{10,1... | collective-permute-start | bytes 392 | tf_op jit(solution)/shard_map/while/body/eval_jaxpr/ppermute | solution.py:11
  58.5 1.1 collective-permute-done.2
  59.6 1.3 %collective-permute-done.3 = f32[32]{0:T(128)S(1)} collective-permute-done((f32[32]{0:T(128)S(1)}, f32[32]{0:T(128)S(1)}, u32[]{:S(2)}, u32[]{:S(2)}) %collective-permute-start.3) | collective-permute-done | bytes 160 | tf_op jit(solution)/shard_map/while/body/eval_jaxpr/ppermute | solution.py:11
  60.9 2.3 %collective-permute-done.4 = f32[32]{0:T(128)S(1)} collective-permute-done((f32[32]{0:T(128)S(1)}, f32[32]{0:T(128)S(1)}, u32[]{:S(2)}, u32[]{:S(2)}) %collective-permute-start.4) | collective-permute-done | bytes 160 | tf_op jit(solution)/shard_map/while/body/eval_jaxpr/ppermute | solution.py:11
  63.3 4.6 %fusion.22 = (f32[32]{0:T(128)S(1)}, f32[32,1024]{1,0:T(8,128)S(1)}) fusion(bf16[32,3584]{1,0:T(8,128)(2,1)S(1)} %copy.14, bf16[3584,1024]{1,0:T(8,128)(2,1)} %get-tuple-element.271), kind=kOutput, calls=%fused_computation.24.clone.1 | convolution fusion | flops 234913760 | bytes 7700608 | tf_op jit(solution)/shard_map/while/body/eval_jaxpr/dot_general | solution.py:23
  68.0 0.2 select_reduce_fusion.3
  68.3 0.2 collective-permute-start.3
  68.5 4.2 %collective-permute-done.2 = f32[32]{0:T(128)S(1)} collective-permute-done((f32[32]{0:T(128)S(1)}, f32[32]{0:T(128)S(1)}, u32[]{:S(2)}, u32[]{:S(2)}) %collective-permute-start.2) | collective-permute-done | bytes 160 | tf_op jit(solution)/shard_map/while/body/eval_jaxpr/ppermute | solution.py:11
  72.7 0.4 collective-permute-done.3
  73.1 0.2 collective-permute-done.4
  73.4 4.6 %fusion.22 = (f32[32]{0:T(128)S(1)}, f32[32,1024]{1,0:T(8,128)S(1)}) fusion(bf16[32,3584]{1,0:T(8,128)(2,1)S(1)} %copy.14, bf16[3584,1024]{1,0:T(8,128)(2,1)} %get-tuple-element.271), kind=kOutput, calls=%fused_computation.24.clone.1 | convolution fusion | flops 234913760 | bytes 7700608 | tf_op jit(solution)/shard_map/while/body/eval_jaxpr/dot_general | solution.py:23
  78.0 1.0 collective-permute-start.1
  79.0 0.2 select_reduce_fusion.3
  79.3 2.3 %collective-permute-start.3 = (f32[32]{0:T(128)S(1)}, f32[32]{0:T(128)S(1)}, u32[]{:S(2)}, u32[]{:S(2)}) collective-permute-start(f32[32]{0:T(128)S(1)} %multiply_add_fusion.3), channel_id=1, source_target_pairs={{0,1},{1,2},{2,3},{3,4},{4,5},{5,6},{6,7},{7,0},{8,9},{9,10},{10,1... | collective-permute-start | bytes 392 | tf_op jit(solution)/shard_map/while/body/eval_jaxpr/ppermute | solution.py:11
  81.7 1.1 collective-permute-done.2
  82.8 1.3 %collective-permute-done.3 = f32[32]{0:T(128)S(1)} collective-permute-done((f32[32]{0:T(128)S(1)}, f32[32]{0:T(128)S(1)}, u32[]{:S(2)}, u32[]{:S(2)}) %collective-permute-start.3) | collective-permute-done | bytes 160 | tf_op jit(solution)/shard_map/while/body/eval_jaxpr/ppermute | solution.py:11
  84.1 2.3 %collective-permute-done.4 = f32[32]{0:T(128)S(1)} collective-permute-done((f32[32]{0:T(128)S(1)}, f32[32]{0:T(128)S(1)}, u32[]{:S(2)}, u32[]{:S(2)}) %collective-permute-start.4) | collective-permute-done | bytes 160 | tf_op jit(solution)/shard_map/while/body/eval_jaxpr/ppermute | solution.py:11
  86.4 4.6 %fusion.11 = (f32[32]{0:T(128)S(1)}, f32[32,1024]{1,0:T(8,128)S(1)}) fusion(bf16[32,3584]{1,0:T(8,128)(2,1)S(1)} %get-tuple-element.88, bf16[3584,1024]{1,0:T(8,128)(2,1)} %get-tuple-element.298), kind=kOutput, calls=%fused_computation.25 | convolution fusion | flops 234913760 | bytes 7700608 | tf_op jit(solution)/shard_map/dot_general | solution.py:23
  91.1 0.2 select_reduce_fusion.1
  91.5 0.1 convert_reduce_fusion
  91.6 0.6 dynamic-slice
  92.8 3.4 %collective-permute-done.6 = f32[32]{0:T(128)S(1)} collective-permute-done((f32[32]{0:T(128)S(1)}, f32[32]{0:T(128)S(1)}, u32[]{:S(2)}, u32[]{:S(2)}) %collective-permute-start.6) | collective-permute-done | bytes 160 | tf_op jit(solution)/shard_map/ppermute | solution.py:11
  96.2 0.2 dynamic-update-slice.1
  96.4 0.2 dynamic-update-slice.2
  96.6 0.2 dynamic-update-slice
  96.8 9.9 %all-reduce.4 = (f32[128]{0:T(128)S(1)}, f32[128]{0:T(128)S(1)}, f32[128]{0:T(128)S(1)}) all-reduce(f32[128]{0:T(128)S(1)} %dynamic-update-slice, f32[128]{0:T(128)S(1)} %dynamic-update-slice.1, f32[128]{0:T(128)S(1)} %dynamic-update-slice.2), channel_id=2, replica_groups=mesh['blk'=4,'tok'=8] {'blk'}, use_global_device_ids=true, to_apply=%add | all-reduce | flops 384 | bytes 3072
  106.8 0.1 reshape.26
  106.9 0.1 reshape.27
  107.2 0.1 while.33
  107.3 0.2 convolution_bitcast_fusion
  107.5 13.6 %all-reduce.3 = (f32[128]{0:T(128)S(1)}, f32[128]{0:T(128)S(1)}) all-reduce(f32[128]{0:T(128)S(1)} %convolution_bitcast_fusion, f32[128]{0:T(128)S(1)} %convert_reduce_fusion), channel_id=1, replica_groups=mesh['blk'=4,'tok'=8] {'tok'}, use_global_device_ids=true, to_apply=%region_10.11 | all-reduce | flops 256 | bytes 2048 | tf_op jit(solution)/shard_map/psum | solution.py:78
  121.1 0.5 div.3
  (118 shorter events, 2.5 us)
Async XLA Ops:
  2.3 14.6 %collective-permute-start = (bf16[32,3584]{1,0:T(8,128)(2,1)S(1)}, bf16[32,3584]{1,0:T(8,128)(2,1)S(1)}, u32[]{:S(2)}, u32[]{:S(2)}) collective-permute-start(bf16[32,3584]{1,0:T(8,128)(2,1)S(1)} %copy.14), channel_id=1, source_target_pairs={{0,1},{1,2},{2,3},{3,4},{4,5},{5,6},{6,7},{7,0},{8,9},{9,10},{10,1... | collective-permute-start | bytes 688136 | tf_op jit(solution)/shard_map/while/body/eval_jaxpr/ppermute | solution.py:11
  7.4 5.3 %collective-permute-start.2 = (f32[32]{0:T(128)S(1)}, f32[32]{0:T(128)S(1)}, u32[]{:S(2)}, u32[]{:S(2)}) collective-permute-start(f32[32]{0:T(128)S(1)} %max.13), channel_id=1, source_target_pairs={{0,1},{1,2},{2,3},{3,4},{4,5},{5,6},{6,7},{7,0},{8,9},{9,10},{10,1... | collective-permute-start | bytes 392 | tf_op jit(solution)/shard_map/while/body/eval_jaxpr/ppermute | solution.py:11
  10.1 6.8 %collective-permute-start.1 = (s32[32]{0:T(128)S(1)}, s32[32]{0:T(128)S(1)}, u32[]{:S(2)}, u32[]{:S(2)}) collective-permute-start(s32[32]{0:T(128)S(1)} %copy.15), channel_id=1, source_target_pairs={{0,1},{1,2},{2,3},{3,4},{4,5},{5,6},{6,7},{7,0},{8,9},{9,10},{10,1... | collective-permute-start | bytes 392 | tf_op jit(solution)/shard_map/while/body/eval_jaxpr/ppermute | solution.py:11
  10.4 4.8 %collective-permute-start.3 = (f32[32]{0:T(128)S(1)}, f32[32]{0:T(128)S(1)}, u32[]{:S(2)}, u32[]{:S(2)}) collective-permute-start(f32[32]{0:T(128)S(1)} %multiply_add_fusion.3), channel_id=1, source_target_pairs={{0,1},{1,2},{2,3},{3,4},{4,5},{5,6},{6,7},{7,0},{8,9},{9,10},{10,1... | collective-permute-start | bytes 392 | tf_op jit(solution)/shard_map/while/body/eval_jaxpr/ppermute | solution.py:11
  12.1 4.8 %collective-permute-start.4 = (f32[32]{0:T(128)S(1)}, f32[32]{0:T(128)S(1)}, u32[]{:S(2)}, u32[]{:S(2)}) collective-permute-start(f32[32]{0:T(128)S(1)} %add.86), channel_id=1, source_target_pairs={{0,1},{1,2},{2,3},{3,4},{4,5},{5,6},{6,7},{7,0},{8,9},{9,10},{10,1... | collective-permute-start | bytes 392 | tf_op jit(solution)/shard_map/while/body/eval_jaxpr/ppermute | solution.py:11
  16.9 10.0 %collective-permute-start = (bf16[32,3584]{1,0:T(8,128)(2,1)S(1)}, bf16[32,3584]{1,0:T(8,128)(2,1)S(1)}, u32[]{:S(2)}, u32[]{:S(2)}) collective-permute-start(bf16[32,3584]{1,0:T(8,128)(2,1)S(1)} %copy.14), channel_id=1, source_target_pairs={{0,1},{1,2},{2,3},{3,4},{4,5},{5,6},{6,7},{7,0},{8,9},{9,10},{10,1... | collective-permute-start | bytes 688136 | tf_op jit(solution)/shard_map/while/body/eval_jaxpr/ppermute | solution.py:11
  21.5 4.8 %collective-permute-start.2 = (f32[32]{0:T(128)S(1)}, f32[32]{0:T(128)S(1)}, u32[]{:S(2)}, u32[]{:S(2)}) collective-permute-start(f32[32]{0:T(128)S(1)} %max.13), channel_id=1, source_target_pairs={{0,1},{1,2},{2,3},{3,4},{4,5},{5,6},{6,7},{7,0},{8,9},{9,10},{10,1... | collective-permute-start | bytes 392 | tf_op jit(solution)/shard_map/while/body/eval_jaxpr/ppermute | solution.py:11
  21.6 5.3 %collective-permute-start.1 = (s32[32]{0:T(128)S(1)}, s32[32]{0:T(128)S(1)}, u32[]{:S(2)}, u32[]{:S(2)}) collective-permute-start(s32[32]{0:T(128)S(1)} %copy.15), channel_id=1, source_target_pairs={{0,1},{1,2},{2,3},{3,4},{4,5},{5,6},{6,7},{7,0},{8,9},{9,10},{10,1... | collective-permute-start | bytes 392 | tf_op jit(solution)/shard_map/while/body/eval_jaxpr/ppermute | solution.py:11
  21.9 4.8 %collective-permute-start.3 = (f32[32]{0:T(128)S(1)}, f32[32]{0:T(128)S(1)}, u32[]{:S(2)}, u32[]{:S(2)}) collective-permute-start(f32[32]{0:T(128)S(1)} %multiply_add_fusion.3), channel_id=1, source_target_pairs={{0,1},{1,2},{2,3},{3,4},{4,5},{5,6},{6,7},{7,0},{8,9},{9,10},{10,1... | collective-permute-start | bytes 392 | tf_op jit(solution)/shard_map/while/body/eval_jaxpr/ppermute | solution.py:11
  22.0 4.9 %collective-permute-start.4 = (f32[32]{0:T(128)S(1)}, f32[32]{0:T(128)S(1)}, u32[]{:S(2)}, u32[]{:S(2)}) collective-permute-start(f32[32]{0:T(128)S(1)} %add.86), channel_id=1, source_target_pairs={{0,1},{1,2},{2,3},{3,4},{4,5},{5,6},{6,7},{7,0},{8,9},{9,10},{10,1... | collective-permute-start | bytes 392 | tf_op jit(solution)/shard_map/while/body/eval_jaxpr/ppermute | solution.py:11
  26.9 13.1 %collective-permute-start = (bf16[32,3584]{1,0:T(8,128)(2,1)S(1)}, bf16[32,3584]{1,0:T(8,128)(2,1)S(1)}, u32[]{:S(2)}, u32[]{:S(2)}) collective-permute-start(bf16[32,3584]{1,0:T(8,128)(2,1)S(1)} %copy.14), channel_id=1, source_target_pairs={{0,1},{1,2},{2,3},{3,4},{4,5},{5,6},{6,7},{7,0},{8,9},{9,10},{10,1... | collective-permute-start | bytes 688136 | tf_op jit(solution)/shard_map/while/body/eval_jaxpr/ppermute | solution.py:11
  31.6 4.8 %collective-permute-start.2 = (f32[32]{0:T(128)S(1)}, f32[32]{0:T(128)S(1)}, u32[]{:S(2)}, u32[]{:S(2)}) collective-permute-start(f32[32]{0:T(128)S(1)} %max.13), channel_id=1, source_target_pairs={{0,1},{1,2},{2,3},{3,4},{4,5},{5,6},{6,7},{7,0},{8,9},{9,10},{10,1... | collective-permute-start | bytes 392 | tf_op jit(solution)/shard_map/while/body/eval_jaxpr/ppermute | solution.py:11
  31.7 8.4 %collective-permute-start.1 = (s32[32]{0:T(128)S(1)}, s32[32]{0:T(128)S(1)}, u32[]{:S(2)}, u32[]{:S(2)}) collective-permute-start(s32[32]{0:T(128)S(1)} %copy.15), channel_id=1, source_target_pairs={{0,1},{1,2},{2,3},{3,4},{4,5},{5,6},{6,7},{7,0},{8,9},{9,10},{10,1... | collective-permute-start | bytes 392 | tf_op jit(solution)/shard_map/while/body/eval_jaxpr/ppermute | solution.py:11
  32.9 4.8 %collective-permute-start.3 = (f32[32]{0:T(128)S(1)}, f32[32]{0:T(128)S(1)}, u32[]{:S(2)}, u32[]{:S(2)}) collective-permute-start(f32[32]{0:T(128)S(1)} %multiply_add_fusion.3), channel_id=1, source_target_pairs={{0,1},{1,2},{2,3},{3,4},{4,5},{5,6},{6,7},{7,0},{8,9},{9,10},{10,1... | collective-permute-start | bytes 392 | tf_op jit(solution)/shard_map/while/body/eval_jaxpr/ppermute | solution.py:11
  35.2 4.8 %collective-permute-start.4 = (f32[32]{0:T(128)S(1)}, f32[32]{0:T(128)S(1)}, u32[]{:S(2)}, u32[]{:S(2)}) collective-permute-start(f32[32]{0:T(128)S(1)} %add.86), channel_id=1, source_target_pairs={{0,1},{1,2},{2,3},{3,4},{4,5},{5,6},{6,7},{7,0},{8,9},{9,10},{10,1... | collective-permute-start | bytes 392 | tf_op jit(solution)/shard_map/while/body/eval_jaxpr/ppermute | solution.py:11
  40.1 10.0 %collective-permute-start = (bf16[32,3584]{1,0:T(8,128)(2,1)S(1)}, bf16[32,3584]{1,0:T(8,128)(2,1)S(1)}, u32[]{:S(2)}, u32[]{:S(2)}) collective-permute-start(bf16[32,3584]{1,0:T(8,128)(2,1)S(1)} %copy.14), channel_id=1, source_target_pairs={{0,1},{1,2},{2,3},{3,4},{4,5},{5,6},{6,7},{7,0},{8,9},{9,10},{10,1... | collective-permute-start | bytes 688136 | tf_op jit(solution)/shard_map/while/body/eval_jaxpr/ppermute | solution.py:11
  44.7 4.8 %collective-permute-start.2 = (f32[32]{0:T(128)S(1)}, f32[32]{0:T(128)S(1)}, u32[]{:S(2)}, u32[]{:S(2)}) collective-permute-start(f32[32]{0:T(128)S(1)} %max.13), channel_id=1, source_target_pairs={{0,1},{1,2},{2,3},{3,4},{4,5},{5,6},{6,7},{7,0},{8,9},{9,10},{10,1... | collective-permute-start | bytes 392 | tf_op jit(solution)/shard_map/while/body/eval_jaxpr/ppermute | solution.py:11
  44.8 5.3 %collective-permute-start.1 = (s32[32]{0:T(128)S(1)}, s32[32]{0:T(128)S(1)}, u32[]{:S(2)}, u32[]{:S(2)}) collective-permute-start(s32[32]{0:T(128)S(1)} %copy.15), channel_id=1, source_target_pairs={{0,1},{1,2},{2,3},{3,4},{4,5},{5,6},{6,7},{7,0},{8,9},{9,10},{10,1... | collective-permute-start | bytes 392 | tf_op jit(solution)/shard_map/while/body/eval_jaxpr/ppermute | solution.py:11
  45.1 4.8 %collective-permute-start.3 = (f32[32]{0:T(128)S(1)}, f32[32]{0:T(128)S(1)}, u32[]{:S(2)}, u32[]{:S(2)}) collective-permute-start(f32[32]{0:T(128)S(1)} %multiply_add_fusion.3), channel_id=1, source_target_pairs={{0,1},{1,2},{2,3},{3,4},{4,5},{5,6},{6,7},{7,0},{8,9},{9,10},{10,1... | collective-permute-start | bytes 392 | tf_op jit(solution)/shard_map/while/body/eval_jaxpr/ppermute | solution.py:11
  45.3 4.8 %collective-permute-start.4 = (f32[32]{0:T(128)S(1)}, f32[32]{0:T(128)S(1)}, u32[]{:S(2)}, u32[]{:S(2)}) collective-permute-start(f32[32]{0:T(128)S(1)} %add.86), channel_id=1, source_target_pairs={{0,1},{1,2},{2,3},{3,4},{4,5},{5,6},{6,7},{7,0},{8,9},{9,10},{10,1... | collective-permute-start | bytes 392 | tf_op jit(solution)/shard_map/while/body/eval_jaxpr/ppermute | solution.py:11
  50.1 13.1 %collective-permute-start = (bf16[32,3584]{1,0:T(8,128)(2,1)S(1)}, bf16[32,3584]{1,0:T(8,128)(2,1)S(1)}, u32[]{:S(2)}, u32[]{:S(2)}) collective-permute-start(bf16[32,3584]{1,0:T(8,128)(2,1)S(1)} %copy.14), channel_id=1, source_target_pairs={{0,1},{1,2},{2,3},{3,4},{4,5},{5,6},{6,7},{7,0},{8,9},{9,10},{10,1... | collective-permute-start | bytes 688136 | tf_op jit(solution)/shard_map/while/body/eval_jaxpr/ppermute | solution.py:11
  54.8 4.8 %collective-permute-start.2 = (f32[32]{0:T(128)S(1)}, f32[32]{0:T(128)S(1)}, u32[]{:S(2)}, u32[]{:S(2)}) collective-permute-start(f32[32]{0:T(128)S(1)} %max.13), channel_id=1, source_target_pairs={{0,1},{1,2},{2,3},{3,4},{4,5},{5,6},{6,7},{7,0},{8,9},{9,10},{10,1... | collective-permute-start | bytes 392 | tf_op jit(solution)/shard_map/while/body/eval_jaxpr/ppermute | solution.py:11
  54.8 8.4 %collective-permute-start.1 = (s32[32]{0:T(128)S(1)}, s32[32]{0:T(128)S(1)}, u32[]{:S(2)}, u32[]{:S(2)}) collective-permute-start(s32[32]{0:T(128)S(1)} %copy.15), channel_id=1, source_target_pairs={{0,1},{1,2},{2,3},{3,4},{4,5},{5,6},{6,7},{7,0},{8,9},{9,10},{10,1... | collective-permute-start | bytes 392 | tf_op jit(solution)/shard_map/while/body/eval_jaxpr/ppermute | solution.py:11
  56.1 4.8 %collective-permute-start.3 = (f32[32]{0:T(128)S(1)}, f32[32]{0:T(128)S(1)}, u32[]{:S(2)}, u32[]{:S(2)}) collective-permute-start(f32[32]{0:T(128)S(1)} %multiply_add_fusion.3), channel_id=1, source_target_pairs={{0,1},{1,2},{2,3},{3,4},{4,5},{5,6},{6,7},{7,0},{8,9},{9,10},{10,1... | collective-permute-start | bytes 392 | tf_op jit(solution)/shard_map/while/body/eval_jaxpr/ppermute | solution.py:11
  58.4 4.8 %collective-permute-start.4 = (f32[32]{0:T(128)S(1)}, f32[32]{0:T(128)S(1)}, u32[]{:S(2)}, u32[]{:S(2)}) collective-permute-start(f32[32]{0:T(128)S(1)} %add.86), channel_id=1, source_target_pairs={{0,1},{1,2},{2,3},{3,4},{4,5},{5,6},{6,7},{7,0},{8,9},{9,10},{10,1... | collective-permute-start | bytes 392 | tf_op jit(solution)/shard_map/while/body/eval_jaxpr/ppermute | solution.py:11
  63.2 10.0 %collective-permute-start = (bf16[32,3584]{1,0:T(8,128)(2,1)S(1)}, bf16[32,3584]{1,0:T(8,128)(2,1)S(1)}, u32[]{:S(2)}, u32[]{:S(2)}) collective-permute-start(bf16[32,3584]{1,0:T(8,128)(2,1)S(1)} %copy.14), channel_id=1, source_target_pairs={{0,1},{1,2},{2,3},{3,4},{4,5},{5,6},{6,7},{7,0},{8,9},{9,10},{10,1... | collective-permute-start | bytes 688136 | tf_op jit(solution)/shard_map/while/body/eval_jaxpr/ppermute | solution.py:11
  67.9 4.8 %collective-permute-start.2 = (f32[32]{0:T(128)S(1)}, f32[32]{0:T(128)S(1)}, u32[]{:S(2)}, u32[]{:S(2)}) collective-permute-start(f32[32]{0:T(128)S(1)} %max.13), channel_id=1, source_target_pairs={{0,1},{1,2},{2,3},{3,4},{4,5},{5,6},{6,7},{7,0},{8,9},{9,10},{10,1... | collective-permute-start | bytes 392 | tf_op jit(solution)/shard_map/while/body/eval_jaxpr/ppermute | solution.py:11
  68.0 5.3 %collective-permute-start.1 = (s32[32]{0:T(128)S(1)}, s32[32]{0:T(128)S(1)}, u32[]{:S(2)}, u32[]{:S(2)}) collective-permute-start(s32[32]{0:T(128)S(1)} %copy.15), channel_id=1, source_target_pairs={{0,1},{1,2},{2,3},{3,4},{4,5},{5,6},{6,7},{7,0},{8,9},{9,10},{10,1... | collective-permute-start | bytes 392 | tf_op jit(solution)/shard_map/while/body/eval_jaxpr/ppermute | solution.py:11
  68.3 4.8 %collective-permute-start.3 = (f32[32]{0:T(128)S(1)}, f32[32]{0:T(128)S(1)}, u32[]{:S(2)}, u32[]{:S(2)}) collective-permute-start(f32[32]{0:T(128)S(1)} %multiply_add_fusion.3), channel_id=1, source_target_pairs={{0,1},{1,2},{2,3},{3,4},{4,5},{5,6},{6,7},{7,0},{8,9},{9,10},{10,1... | collective-permute-start | bytes 392 | tf_op jit(solution)/shard_map/while/body/eval_jaxpr/ppermute | solution.py:11
  68.5 4.8 %collective-permute-start.4 = (f32[32]{0:T(128)S(1)}, f32[32]{0:T(128)S(1)}, u32[]{:S(2)}, u32[]{:S(2)}) collective-permute-start(f32[32]{0:T(128)S(1)} %add.86), channel_id=1, source_target_pairs={{0,1},{1,2},{2,3},{3,4},{4,5},{5,6},{6,7},{7,0},{8,9},{9,10},{10,1... | collective-permute-start | bytes 392 | tf_op jit(solution)/shard_map/while/body/eval_jaxpr/ppermute | solution.py:11
  73.3 13.1 %collective-permute-start = (bf16[32,3584]{1,0:T(8,128)(2,1)S(1)}, bf16[32,3584]{1,0:T(8,128)(2,1)S(1)}, u32[]{:S(2)}, u32[]{:S(2)}) collective-permute-start(bf16[32,3584]{1,0:T(8,128)(2,1)S(1)} %copy.14), channel_id=1, source_target_pairs={{0,1},{1,2},{2,3},{3,4},{4,5},{5,6},{6,7},{7,0},{8,9},{9,10},{10,1... | collective-permute-start | bytes 688136 | tf_op jit(solution)/shard_map/while/body/eval_jaxpr/ppermute | solution.py:11
  77.9 4.8 %collective-permute-start.2 = (f32[32]{0:T(128)S(1)}, f32[32]{0:T(128)S(1)}, u32[]{:S(2)}, u32[]{:S(2)}) collective-permute-start(f32[32]{0:T(128)S(1)} %max.13), channel_id=1, source_target_pairs={{0,1},{1,2},{2,3},{3,4},{4,5},{5,6},{6,7},{7,0},{8,9},{9,10},{10,1... | collective-permute-start | bytes 392 | tf_op jit(solution)/shard_map/while/body/eval_jaxpr/ppermute | solution.py:11
  78.0 8.4 %collective-permute-start.1 = (s32[32]{0:T(128)S(1)}, s32[32]{0:T(128)S(1)}, u32[]{:S(2)}, u32[]{:S(2)}) collective-permute-start(s32[32]{0:T(128)S(1)} %copy.15), channel_id=1, source_target_pairs={{0,1},{1,2},{2,3},{3,4},{4,5},{5,6},{6,7},{7,0},{8,9},{9,10},{10,1... | collective-permute-start | bytes 392 | tf_op jit(solution)/shard_map/while/body/eval_jaxpr/ppermute | solution.py:11
  79.3 4.8 %collective-permute-start.3 = (f32[32]{0:T(128)S(1)}, f32[32]{0:T(128)S(1)}, u32[]{:S(2)}, u32[]{:S(2)}) collective-permute-start(f32[32]{0:T(128)S(1)} %multiply_add_fusion.3), channel_id=1, source_target_pairs={{0,1},{1,2},{2,3},{3,4},{4,5},{5,6},{6,7},{7,0},{8,9},{9,10},{10,1... | collective-permute-start | bytes 392 | tf_op jit(solution)/shard_map/while/body/eval_jaxpr/ppermute | solution.py:11
  81.6 4.8 %collective-permute-start.4 = (f32[32]{0:T(128)S(1)}, f32[32]{0:T(128)S(1)}, u32[]{:S(2)}, u32[]{:S(2)}) collective-permute-start(f32[32]{0:T(128)S(1)} %add.86), channel_id=1, source_target_pairs={{0,1},{1,2},{2,3},{3,4},{4,5},{5,6},{6,7},{7,0},{8,9},{9,10},{10,1... | collective-permute-start | bytes 392 | tf_op jit(solution)/shard_map/while/body/eval_jaxpr/ppermute | solution.py:11
  86.4 5.1 %copy-start.2 = (s32[32]{0:T(128)S(1)}, s32[32]{0:T(128)}, u32[]{:S(2)}) copy-start(s32[32]{0:T(128)} %param.13) | copy-start | bytes 388
  86.4 5.2 %copy-start.3 = (u32[32]{0:T(128)S(1)}, u32[32]{0:T(128)}, u32[]{:S(2)}) copy-start(u32[32]{0:T(128)} %constant.40) | copy-start | bytes 388
  86.4 20.9 %copy-start = (f32[32]{0:T(128)S(1)}, f32[32]{0:T(128)}, u32[]{:S(2)}) copy-start(f32[32]{0:T(128)} %param.12) | copy-start | bytes 388
  91.0 5.6 %collective-permute-start.5 = (f32[32]{0:T(128)S(1)}, f32[32]{0:T(128)S(1)}, u32[]{:S(2)}, u32[]{:S(2)}) collective-permute-start(f32[32]{0:T(128)S(1)} %max.9), channel_id=1, source_target_pairs={{0,1},{1,2},{2,3},{3,4},{4,5},{5,6},{6,7},{7,0},{8,9},{9,10},{10,1... | collective-permute-start | bytes 392 | tf_op jit(solution)/shard_map/ppermute | solution.py:11
  91.3 4.8 %collective-permute-start.6 = (f32[32]{0:T(128)S(1)}, f32[32]{0:T(128)S(1)}, u32[]{:S(2)}, u32[]{:S(2)}) collective-permute-start(f32[32]{0:T(128)S(1)} %multiply_add_fusion.1), channel_id=1, source_target_pairs={{0,1},{1,2},{2,3},{3,4},{4,5},{5,6},{6,7},{7,0},{8,9},{9,10},{10,1... | collective-permute-start | bytes 392 | tf_op jit(solution)/shard_map/ppermute | solution.py:11
  91.4 5.0 %collective-permute-start.7 = (f32[32]{0:T(128)S(1)}, f32[32]{0:T(128)S(1)}, u32[]{:S(2)}, u32[]{:S(2)}) collective-permute-start(f32[32]{0:T(128)S(1)} %add.58), channel_id=1, source_target_pairs={{0,1},{1,2},{2,3},{3,4},{4,5},{5,6},{6,7},{7,0},{8,9},{9,10},{10,1... | collective-permute-start | bytes 392 | tf_op jit(solution)/shard_map/ppermute | solution.py:11
  107.3 14.3 %copy-start.1 = (f32[32]{0:T(128)}, f32[32]{0:T(128)S(1)}, u32[]{:S(2)}) copy-start(f32[32]{0:T(128)S(1)} %subtract_subtract_fusion) | copy-start | bytes 388
where the time goes:
time: 122 us
  matrix products  36.6 us (30%)
  waiting for transfers between devices  36.5 us (30%)
  blocking collectives  23.5 us (19%)
  starting transfers between devices  17.1 us (14%)
  local copies, waits for them, and re-layouts  3.47 us (3%)
  other arithmetic  2.56 us (2%)
  between operations  1.41 us (1%)
    ppermute x38, waiting for transfers between devices, from_behind(): lax.ppermute(value, axis, [(i, (i + by) % devices) for i in range(devices)])  36.5 us
    dot_general x8, matrix products, absorb(): logits = jnp.dot(token_rows, head, preferred_element_type=jnp.float32)  36.5 us
    ppermute x38, starting transfers between devices, from_behind(): lax.ppermute(value, axis, [(i, (i + by) % devices) for i in range(devices)])  17.1 us
    psum x1, blocking collectives, on_device(): totals, counts = lax.psum((totals, counts), 'tok')  13.6 us
    unnamed x1, blocking collectives  9.88 us
    unnamed x17, local copies, waits for them, and re-layouts  2.86 us
  transfers between devices with their start and end apart: 38, of which 22 were waited for; matrix products, arithmetic and copies ran while one was open for 29% of the time, Pallas kernels for 0%

commit v1 on v0

v1 whole, which is shorter than its diff:
```python
import functools

import jax
import jax.numpy as jnp
from jax import lax
from jax.experimental import pallas as pl
from jax.experimental.pallas import tpu as pltpu
from jax.sharding import PartitionSpec as P

quarters = 4
lanes = 128


def flipped(index, bits):
    bit = 1
    result = index
    while bit <= bits:
        if bits & bit:
            result = result + bit - 2 * bit * lax.rem(lax.div(index, bit), 2)
        bit = 2 * bit
    return result


def kernel(
    blks, toks, states, head, targets, ref_loss, seq_ids, excess_out, score_out,
    rows, weights, logits, meta, columns, stats,
    states_sem, head_sem, send_sem, z_sem, side_sem, half_sem, core_sem, own_sem,
    meta_send, meta_recv, stats_send, stats_recv,
):
    blk, tok = lax.axis_index("blk"), lax.axis_index("tok")
    local = states.shape[0]
    depth = weights.shape[1]
    width = weights.shape[2]
    tokens = toks * local
    seqs = score_out.shape[1]
    chips = toks // 2
    devices = blks * toks
    me = blk * toks + tok
    mine = lax.rem(blk, quarters)
    partner = flipped(tok, 1)

    def place(owner, begin=0, size=local):
        return pl.ds(pl.multiple_of(owner * local + begin, 16), size)

    def send(source, target, sent, received, to_blk, to_tok):
        pltpu.make_async_remote_copy(
            src_ref=source, dst_ref=target, send_sem=sent, recv_sem=received,
            device_id={"blk": to_blk, "tok": to_tok},
            device_id_type=pl.DeviceIdType.MESH,
        ).start()

    def pass_on(part, received, to_blk, to_tok):
        send(part, part, send_sem, received, to_blk, to_tok)

    def arrived(part, received):
        pltpu.make_async_copy(part, part, received).wait()

    states_in = []
    for step in range(quarters):
        part = flipped(mine, step)
        states_in.append(pltpu.make_async_copy(
            states.at[:, pl.ds(pl.multiple_of(part * depth, lanes), depth)],
            rows.at[part, place(tok)], states_sem.at[step]))
        states_in[-1].start()
    head_in = []
    for step in range(quarters):
        part = flipped(mine, step)
        head_in.append(pltpu.make_async_copy(
            head.at[pl.ds(pl.multiple_of(part * depth, 16), depth)],
            weights.at[part], head_sem.at[step]))
        head_in[-1].start()

    barrier = pltpu.get_barrier_semaphore()
    greeted = [(blk, flipped(tok, step)) for step in range(1, toks)]
    greeted += [(flipped(blk, 1), tok), (flipped(blk, 2), tok)]
    for to_blk, to_tok in greeted:
        pl.semaphore_signal(
            barrier, inc=1, device_id={"blk": to_blk, "tok": to_tok},
            device_id_type=pl.DeviceIdType.MESH)
    meta[tok] = jnp.zeros((8, lanes), jnp.float32)
    meta[tok, 0:1, 0:local] = targets[...].astype(jnp.float32)
    meta[tok, 1:2, 0:local] = ref_loss[...]
    meta[tok, 2:3, 0:local] = seq_ids[...].astype(jnp.float32)
    states_in[0].wait()
    pl.semaphore_wait(barrier, len(greeted))

    for step in range(1, chips):
        pass_on(rows.at[mine, place(tok)], z_sem.at[step], blk, flipped(tok, 2 * step))
    for step in range(1, toks):
        send(meta.at[tok], meta.at[tok], meta_send, meta_recv, blk, flipped(tok, step))
    for step in range(1, quarters):
        states_in[step].wait()
    pass_on(rows.at[:, place(tok)], own_sem.at[0], blk, partner)

    def piece(part, step, begin=0, size=local, core=0):
        return rows.at[flipped(mine, part), place(flipped(tok, 2 * step + core), begin, size)]

    half = local // 2

    def forward_z(step):
        arrived(piece(0, step), z_sem.at[step])
        pass_on(piece(0, step), side_sem.at[0, step], flipped(blk, 1), tok)
        pass_on(piece(0, step), side_sem.at[1, step], flipped(blk, 2), tok)
        pass_on(piece(0, step), core_sem.at[0, step], blk, partner)

    def forward_sides(step):
        for side in (0, 1):
            part = side + 1
            arrived(piece(part, step), side_sem.at[side, step])
            pass_on(piece(part, step, side * half, half), half_sem.at[side, step],
                    flipped(blk, 3 - part), tok)
            pass_on(piece(part, step), core_sem.at[part, step], blk, partner)

    def forward_halves(step):
        for side in (0, 1):
            arrived(piece(3, step, side * half, half), half_sem.at[side, step])
            pass_on(piece(3, step, side * half, half), core_sem.at[3 + side, step], blk, partner)

    def multiply(part):
        for step in range(1, chips):
            if part < 3:
                arrived(piece(part, step, core=1), core_sem.at[part, step])
            else:
                for side in (0, 1):
                    arrived(piece(part, step, side * half, half, core=1),
                            core_sem.at[3 + side, step])
        head_in[part].wait()
        at = flipped(mine, part)
        block = min(tokens, 256)

        def one(index):
            here = pl.ds(pl.multiple_of(index * block, block), block)
            product = jnp.dot(rows[at, here], weights[at], preferred_element_type=jnp.float32)
            logits[here] = product if part == 0 else logits[here] + product

        if block == tokens:
            one(0)
        else:
            pl.loop(0, tokens // block)(one)

    jobs = []
    for step in range(1, chips):
        jobs.append((3 * step, forward_z, step))
        jobs.append((3 * step + 4, forward_sides, step))
        jobs.append((3 * step + 8, forward_halves, step))
    last = 3 * (chips - 1)
    jobs = sorted(jobs, key=lambda job: job[0])
    multiplied = 0
    for when, job, step in jobs:
        if when > last + 4 and multiplied == 0:
            arrived(rows.at[:, place(partner)], own_sem.at[0])
            arrived(meta.at[pl.ds(0, toks - 1)], meta_recv)
            multiply(0)
            multiplied = 1
        job(step)
    for part in range(multiplied, quarters):
        if part == 0:
            arrived(rows.at[:, place(partner)], own_sem.at[0])
            arrived(meta.at[pl.ds(0, toks - 1)], meta_recv)
        if part == 3:
            for owner in range(toks):
                columns[owner * local:(owner + 1) * local] = meta[owner].T[0:local]
        multiply(part)

    block = min(tokens, 256)
    for begin in range(0, tokens, block):
        here = pl.ds(begin, block)
        values = logits[here]
        highest = jnp.max(values, axis=1, keepdims=True)
        scaled = jnp.sum(jnp.exp(values - highest), axis=1, keepdims=True)
        total = highest + jnp.log(scaled)
        spots = lax.broadcasted_iota(jnp.int32, values.shape, 1) + me * width
        wanted = columns[here, 0:1].astype(jnp.int32)
        picked = jnp.sum(jnp.where(spots == wanted, values, 0.0), axis=1, keepdims=True)
        lane = lax.broadcasted_iota(jnp.int32, (block, lanes), 1)
        packed = jnp.where(lane == 0, total, jnp.where(lane == 1, picked, columns[here, 1:2]))
        turned = packed.T
        stats[devices - 1, :, here] = turned[0:2]
        logits[0:1, here] = turned[2:3]

    def broadcast(by, _):
        to = lax.rem(me + by, devices)
        send(stats.at[devices - 1], stats.at[by - 1], stats_send, stats_recv,
             lax.div(to, toks), lax.rem(to, toks))
        return _

    lax.fori_loop(1, devices, broadcast, 0)

    member = (columns[:, 2:3].astype(jnp.int32)
              == lax.broadcasted_iota(jnp.int32, (tokens, seqs), 1)).astype(jnp.float32)
    own = lax.broadcasted_iota(jnp.int32, (tokens, lanes), 1)
    own = (lax.broadcasted_iota(jnp.int32, (tokens, lanes), 0) == own + tok * local)
    chosen = jnp.concatenate([member, own.astype(jnp.float32)], axis=1)
    loss = logits[0:1, 0:tokens]

    arrived(stats.at[pl.ds(0, devices - 1)], stats_recv)
    gathered = stats[...]
    peak = jnp.max(gathered, axis=0)
    total = peak + jnp.log(jnp.sum(jnp.exp(gathered - peak[None]), axis=0))
    picked = jnp.sum(gathered, axis=0)
    excess = total[0:1] - picked[1:2] - loss
    left = jnp.where(lax.broadcasted_iota(jnp.int32, (8, tokens), 0) == 0, excess, 1.0)
    sums = jnp.dot(left, chosen, precision=lax.Precision.HIGHEST,
                   preferred_element_type=jnp.float32)
    excess_out[...] = sums[0:1, seqs:seqs + local]
    score_out[...] = sums[0:1, 0:seqs] / sums[1:2, 0:seqs]

    arrived(rows.at[:, pl.ds(0, tokens - local)], send_sem)
    arrived(meta.at[pl.ds(0, toks - 1)], meta_send)
    arrived(stats.at[pl.ds(0, devices - 1)], stats_send)


def on_device(states, head, targets, ref_loss, seq_ids):
    blks, toks = lax.axis_size("blk"), lax.axis_size("tok")
    local, model = states.shape
    width = head.shape[1]
    tokens = local * toks
    seqs = tokens // 2
    devices = blks * toks
    depth = model // quarters
    chips = toks // 2
    dma = pltpu.SemaphoreType.DMA
    small = pl.BlockSpec(memory_space=pltpu.VMEM)
    large = pl.BlockSpec(memory_space=pl.ANY)
    excess, score = pl.pallas_call(
        functools.partial(kernel, blks, toks),
        out_shape=(
            jax.ShapeDtypeStruct((1, local), jnp.float32),
            jax.ShapeDtypeStruct((1, seqs), jnp.float32),
        ),
        in_specs=[large, large, small, small, small],
        out_specs=(small, small),
        scratch_shapes=[
            pltpu.VMEM((quarters, tokens, depth), jnp.bfloat16),
            pltpu.VMEM((quarters, depth, width), jnp.bfloat16),
            pltpu.VMEM((tokens, width), jnp.float32),
            pltpu.VMEM((toks, 8, lanes), jnp.float32),
            pltpu.VMEM((tokens, 8), jnp.float32),
            pltpu.VMEM((devices, 2, tokens), jnp.float32),
            dma((quarters,)),
            dma((quarters,)),
            dma,
            dma((chips,)),
            dma((2, chips)),
            dma((2, chips)),
            dma((5, chips)),
            dma((1,)),
            dma, dma, dma, dma,
        ],
        compiler_params=pltpu.CompilerParams(collective_id=0, has_side_effects=True),
    )(states, head, targets.reshape(1, local), ref_loss.reshape(1, local),
      seq_ids.reshape(1, local))
    return excess.reshape(local), score.reshape(seqs)


def solution(mesh):
    placed = (P("tok", None), P(None, ("blk", "tok")), P("tok"), P("tok"), P("tok"))
    return jax.shard_map(
        on_device, mesh=mesh, in_specs=placed, out_specs=(P("tok"), P()), check_vma=False
    )
```

time: 122 us -> 31 us (0.25)
  matrix products: 36.6 us -> 0 us
  waiting for transfers between devices: 36.5 us -> 0 us
  Pallas kernels: 0 us -> 27.9 us
  blocking collectives: 23.5 us -> 0 us
  starting transfers between devices: 17.1 us -> 0 us
  other arithmetic: 2.56 us -> 0 us
  local copies, waits for them, and re-layouts: 3.47 us -> 2.25 us
    dot_general x9 -> x0, matrix products: 36.6 us -> none  [the longest x8 36.5 us: absorb(): logits = jnp.dot(token_rows, head, preferred_element_type=jnp.float32)]
    ppermute x38 -> x0, waiting for transfers between devices: 36.5 us -> none  [from_behind(): lax.ppermute(value, axis, [(i, (i + by) % devices) for i in range(devices)])]
    pallas_call x0 -> x1, Pallas kernels: none -> 27.9 us  [on_device(): pl.pallas_call(functools.partial(kernel, blks, toks), out_shape=(jax.Shap...]
    ppermute x38 -> x0, starting transfers between devices: 17.1 us -> none  [from_behind(): lax.ppermute(value, axis, [(i, (i + by) % devices) for i in range(devices)])]
    psum x1 -> x0, blocking collectives: 13.6 us -> none  [on_device(): totals, counts = lax.psum((totals, counts), 'tok')]
    unnamed x1 -> x0, blocking collectives: 9.88 us -> none
    reduce_sum x9 -> x0, other arithmetic: 1.77 us -> none  [the longest x8 1.68 us: absorb(): picked = picked + jnp.sum(jnp.where(hits, logits, 0.0), axis=1)]
    unnamed x17 -> x2, local copies, waits for them, and re-layouts: 2.86 us -> 2.25 us
  transfers between devices with their start and end apart: 38 -> 0, of which waited for: 22 -> 0; matrix products, arithmetic and copies ran while one was open for 29% -> 0% of each run, Pallas kernels for 0% -> 0%
where the time goes in v1:
time: 31 us; the launch traced here: 30.8 us
  Pallas kernels  27.9 us (90%)
  local copies, waits for them, and re-layouts  2.25 us (7%)
  between operations  0.64 us (2%)
    pallas_call x1, Pallas kernels, on_device(): pl.pallas_call(functools.partial(kernel, blks, toks), out_shape=(jax.Shap...  27.9 us
    unnamed x2, local copies, waits for them, and re-layouts  2.25 us

profile of v1, /device:TPU:0, one launch (start us, length us, event | category | flops | bytes accessed | tf_op | source)
XLA Modules:
  0.0 30.8 jit_solution(841341496944619808)
XLA Ops:
  0.6 27.9 %shard_map.68 = (f32[1,32]{1,0:T(1,128)}, f32[1,128]{1,0:T(1,128)}) custom-call(bf16[32,3584]{1,0:T(8,128)(2,1)} %states.1, bf16[3584,1024]{1,0:T(8,128)(2,1)} %head.1, s32[1,32]{1,0:T(1,128)} %bitcast.5, f32[1,32]{1,0:T(1,128)} %bitcast.6, s32[1,32]{1,0:T(1,128)} %bitcast.7), custom_call_target="tpu_custom_call" | custom-call | tf_op jit(solution)/shard_map/pallas_call | solution.py:225
  28.5 1.1 %copy.9 = f32[32]{0:T(128)} copy(f32[32]{0:T(128)} %bitcast.9) | data formatting | bytes 256
  29.6 1.1 %copy.10 = f32[128]{0:T(128)} copy(f32[128]{0:T(128)} %bitcast.8) | data formatting | bytes 1024

commit v2 on v1

--- a/solution.py
+++ b/solution.py
@@ -24,7 +24,7 @@
 def kernel(
     blks, toks, states, head, targets, ref_loss, seq_ids, excess_out, score_out,
     rows, weights, logits, meta, columns, stats,
-    states_sem, head_sem, send_sem, z_sem, side_sem, half_sem, core_sem, own_sem,
+    small_ints, small_floats, states_sem, head_sem, small_sem, send_sem, z_sem, side_sem, half_sem, core_sem, own_sem,
     meta_send, meta_recv, stats_send, stats_recv,
 ):
     blk, tok = lax.axis_index("blk"), lax.axis_index("tok")
@@ -62,6 +62,13 @@
             states.at[:, pl.ds(pl.multiple_of(part * depth, lanes), depth)],
             rows.at[part, place(tok)], states_sem.at[step]))
         states_in[-1].start()
+    small_in = [
+        pltpu.make_async_copy(targets, small_ints.at[0], small_sem.at[0]),
+        pltpu.make_async_copy(ref_loss, small_floats, small_sem.at[1]),
+        pltpu.make_async_copy(seq_ids, small_ints.at[1], small_sem.at[2]),
+    ]
+    for copy in small_in:
+        copy.start()
     head_in = []
     for step in range(quarters):
         part = flipped(mine, step)
@@ -77,53 +84,59 @@
         pl.semaphore_signal(
             barrier, inc=1, device_id={"blk": to_blk, "tok": to_tok},
             device_id_type=pl.DeviceIdType.MESH)
-    meta[tok] = jnp.zeros((8, lanes), jnp.float32)
-    meta[tok, 0:1, 0:local] = targets[...].astype(jnp.float32)
-    meta[tok, 1:2, 0:local] = ref_loss[...]
-    meta[tok, 2:3, 0:local] = seq_ids[...].astype(jnp.float32)
     states_in[0].wait()
     pl.semaphore_wait(barrier, len(greeted))
 
+    half = local // 2
     for step in range(1, chips):
-        pass_on(rows.at[mine, place(tok)], z_sem.at[step], blk, flipped(tok, 2 * step))
+        for cut in (0, 1):
+            pass_on(rows.at[mine, place(tok, cut * half, half)], z_sem.at[step, cut], blk,
+                    flipped(tok, 2 * step))
+    for copy in small_in:
+        copy.wait()
+    meta[tok] = jnp.zeros((8, lanes), jnp.float32)
+    meta[tok, 0:1, 0:local] = small_ints[0].astype(jnp.float32)
+    meta[tok, 1:2, 0:local] = small_floats[...]
+    meta[tok, 2:3, 0:local] = small_ints[1].astype(jnp.float32)
+    for step in range(1, quarters):
+        states_in[step].wait()
+    for cut in (0, 1):
+        pass_on(rows.at[flipped(mine, 3), place(tok, cut * half, half)], half_sem.at[1, cut],
+                blk, flipped(tok, 2))
+    pass_on(rows.at[:, place(tok)], own_sem.at[0], blk, partner)
+
     for step in range(1, toks):
         send(meta.at[tok], meta.at[tok], meta_send, meta_recv, blk, flipped(tok, step))
-    for step in range(1, quarters):
-        states_in[step].wait()
-    pass_on(rows.at[:, place(tok)], own_sem.at[0], blk, partner)
 
     def piece(part, step, begin=0, size=local, core=0):
         return rows.at[flipped(mine, part), place(flipped(tok, 2 * step + core), begin, size)]
 
-    half = local // 2
-
-    def forward_z(step):
-        arrived(piece(0, step), z_sem.at[step])
-        pass_on(piece(0, step), side_sem.at[0, step], flipped(blk, 1), tok)
-        pass_on(piece(0, step), side_sem.at[1, step], flipped(blk, 2), tok)
-        pass_on(piece(0, step), core_sem.at[0, step], blk, partner)
-
-    def forward_sides(step):
-        for side in (0, 1):
+    def forward_z(step, cut):
+        here = piece(0, step, cut * half, half)
+        arrived(here, z_sem.at[step, cut])
+        pass_on(here, side_sem.at[0, step, cut], flipped(blk, 1), tok)
+        pass_on(here, side_sem.at[1, step, cut], flipped(blk, 2), tok)
+        pass_on(here, core_sem.at[0, step, cut], blk, partner)
+
+    def forward_sides(step, cut):
+        for side in (cut, 1 - cut):
             part = side + 1
-            arrived(piece(part, step), side_sem.at[side, step])
-            pass_on(piece(part, step, side * half, half), half_sem.at[side, step],
-                    flipped(blk, 3 - part), tok)
-            pass_on(piece(part, step), core_sem.at[part, step], blk, partner)
-
-    def forward_halves(step):
-        for side in (0, 1):
-            arrived(piece(3, step, side * half, half), half_sem.at[side, step])
-            pass_on(piece(3, step, side * half, half), core_sem.at[3 + side, step], blk, partner)
+            here = piece(part, step, cut * half, half)
+            arrived(here, side_sem.at[side, step, cut])
+            if side == cut and step > 1:
+                pass_on(here, half_sem.at[step, cut], flipped(blk, 3 - part), tok)
+            pass_on(here, core_sem.at[part, step, cut], blk, partner)
+
+    def forward_halves(step, cut):
+        here = piece(3, step, cut * half, half)
+        arrived(here, half_sem.at[step, cut])
+        pass_on(here, core_sem.at[3, step, cut], blk, partner)
 
     def multiply(part):
         for step in range(1, chips):
-            if part < 3:
-                arrived(piece(part, step, core=1), core_sem.at[part, step])
-            else:
-                for side in (0, 1):
-                    arrived(piece(part, step, side * half, half, core=1),
-                            core_sem.at[3 + side, step])
+            for cut in (0, 1):
+                arrived(piece(part, step, cut * half, half, core=1),
+                        core_sem.at[part, step, cut])
         head_in[part].wait()
         at = flipped(mine, part)
         block = min(tokens, 256)
@@ -139,25 +152,23 @@
             pl.loop(0, tokens // block)(one)
 
     jobs = []
-    for step in range(1, chips):
-        jobs.append((3 * step, forward_z, step))
-        jobs.append((3 * step + 4, forward_sides, step))
-        jobs.append((3 * step + 8, forward_halves, step))
-    last = 3 * (chips - 1)
+    for order in range(2 * (chips - 1)):
+        spot = (1 + order // 2, order % 2)
+        jobs.append((7 * order, forward_z, spot))
+        jobs.append((7 * order + 23, forward_sides, spot))
+        jobs.append((7 * order + 45, forward_halves, spot))
     jobs = sorted(jobs, key=lambda job: job[0])
-    multiplied = 0
-    for when, job, step in jobs:
-        if when > last + 4 and multiplied == 0:
-            arrived(rows.at[:, place(partner)], own_sem.at[0])
-            arrived(meta.at[pl.ds(0, toks - 1)], meta_recv)
-            multiply(0)
-            multiplied = 1
-        job(step)
-    for part in range(multiplied, quarters):
+    last = 7 * (2 * chips - 3)
+    cuts = [last + 23, last + 31, last + 38, last + 45]
+    low = -1
+    for part in range(quarters):
+        for when, job, spot in jobs:
+            if low < when <= cuts[part]:
+                job(*spot)
+        low = cuts[part]
         if part == 0:
             arrived(rows.at[:, place(partner)], own_sem.at[0])
             arrived(meta.at[pl.ds(0, toks - 1)], meta_recv)
-        if part == 3:
             for owner in range(toks):
                 columns[owner * local:(owner + 1) * local] = meta[owner].T[0:local]
         multiply(part)
@@ -225,10 +236,10 @@
     excess, score = pl.pallas_call(
         functools.partial(kernel, blks, toks),
         out_shape=(
-            jax.ShapeDtypeStruct((1, local), jnp.float32),
-            jax.ShapeDtypeStruct((1, seqs), jnp.float32),
+            pltpu.VMEM((1, local), jnp.float32),
+            pltpu.VMEM((1, seqs), jnp.float32),
         ),
-        in_specs=[large, large, small, small, small],
+        in_specs=[large] * 5,
         out_specs=(small, small),
         scratch_shapes=[
             pltpu.VMEM((quarters, tokens, depth), jnp.bfloat16),
@@ -237,13 +248,16 @@
             pltpu.VMEM((toks, 8, lanes), jnp.float32),
             pltpu.VMEM((tokens, 8), jnp.float32),
             pltpu.VMEM((devices, 2, tokens), jnp.float32),
+            pltpu.VMEM((2, 1, local), jnp.int32),
+            pltpu.VMEM((1, local), jnp.float32),
             dma((quarters,)),
             dma((quarters,)),
+            dma((3,)),
             dma,
-            dma((chips,)),
-            dma((2, chips)),
-            dma((2, chips)),
-            dma((5, chips)),
+            dma((chips, 2)),
+            dma((2, chips, 2)),
+            dma((chips, 2)),
+            dma((4, chips, 2)),
             dma((1,)),
             dma, dma, dma, dma,
         ],

time: 31 us -> 27.8 us (0.90)
  Pallas kernels: 27.9 us -> 26 us
  local copies, waits for them, and re-layouts: 2.25 us -> 1.02 us
    pallas_call x1, Pallas kernels: 27.9 us -> 26 us  [on_device(): pl.pallas_call(functools.partial(kernel, blks, toks), out_shape=(pltpu.VM...]
    unnamed x2, local copies, waits for them, and re-layouts: 2.25 us -> 1.02 us
where the time goes in v2:
time: 27.8 us; the launch traced here: 27.6 us
  Pallas kernels  26 us (94%)
  local copies, waits for them, and re-layouts  1.02 us (4%)
  between operations  0.64 us (2%)
    pallas_call x1, Pallas kernels, on_device(): pl.pallas_call(functools.partial(kernel, blks, toks), out_shape=(pltpu.VM...  26 us
    unnamed x2, local copies, waits for them, and re-layouts  1.02 us

profile of v2, /device:TPU:0, one launch (start us, length us, event | category | flops | bytes accessed | tf_op | source)
XLA Modules:
  0.0 27.6 jit_solution(6270385054423447622)
XLA Ops:
  0.6 26.0 %shard_map.68 = (f32[1,32]{1,0:T(1,128)S(1)}, f32[1,128]{1,0:T(1,128)S(1)}) custom-call(bf16[32,3584]{1,0:T(8,128)(2,1)} %states.1, bf16[3584,1024]{1,0:T(8,128)(2,1)} %head.1, s32[1,32]{1,0:T(1,128)} %bitcast.7, f32[1,32]{1,0:T(1,128)} %bitcast.8, s32[1,32]{1,0:T(1,128)} %bitcast.9), custom_call_target="tpu_custom_call" | custom-call | tf_op jit(solution)/shard_map/pallas_call | solution.py:236
  26.6 0.5 %copy.9 = f32[32]{0:T(128)} copy(f32[32]{0:T(128)S(1)} %bitcast.6) | data formatting | bytes 256
  27.1 0.5 %copy.10 = f32[128]{0:T(128)} copy(f32[128]{0:T(128)S(1)} %bitcast.5) | data formatting | bytes 1024
